TPU v7x, 512 devices: a whole 4x4x16 slice. The times are simulated.
512 devices in a mesh: blk: 512 (over x, y, z, core).
Axes of the slice: x: 4, y: 4, z: 16, core: 2. Of those that a mesh axis runs over, the one named last changes fastest.
Arguments:
- queries: bfloat16 [32768, 4096], P('blk'), may hold values from -200 to 200
- keys: bfloat16 [32768, 2048], P('blk'), may hold values from -8 to 8
- values: bfloat16 [32768, 2048], P('blk'), may hold values from -6 to 6
- doc_start: int32 [32768], P('blk'), may hold values from 0 to 32767, as said below
Outputs:
- attended: bfloat16 [32768, 4096], P('blk')
Inputs may be any that keep to these rules, and one draw needn't show every extreme that they name: doc_start[i] is the first position of token i's document: nondecreasing, at most i, doc_start[doc_start[i]] = doc_start[i], and position 0 starts a document.
All inputs are finite; a program needn't handle non-finite values.
Results may differ from a plain program's by a relative error of at most 0.0034.
Values may be sent and summed in bfloat16 or wider, within the bound.
A program may use at most 64 MiB of HBM per device.

v0:
```python
from functools import partial

import jax
import jax.numpy as jnp
from jax import lax
from jax.sharding import PartitionSpec as P

HD = 256
HOPS = 4


negative = -1e30


def shifted(block, axis, distance):
    devices = range(lax.axis_size(axis))
    route = [(i - distance, i) for i in devices if i - distance in devices]
    return lax.ppermute(block, axis, route)


def masked_scores(query_part, key_part, starts, q_pos, k_pos, window):
    scores = (
        jnp.einsum("qgrd,kgd->grqk", query_part, key_part, preferred_element_type=jnp.float32)
        * 0.0625
    )
    allowed = (
        (k_pos[None, :] <= q_pos[:, None])
        & (q_pos[:, None] - k_pos[None, :] < window)
        & (k_pos[None, :] >= starts[:, None])
    )
    return jnp.where(allowed, scores, jnp.float32(negative))


def scores_if_seen(seen, query_part, key_part, starts, q_pos, k_pos, window):
    shape = (key_part.shape[1], query_part.shape[2], query_part.shape[0], key_part.shape[0])
    compute = partial(masked_scores, query_part, key_part, starts, q_pos, k_pos, window)
    return lax.cond(seen, compute, lambda: jnp.full(shape, negative, jnp.float32))


def per_device(queries, keys, values, doc_start):
    rows = queries.shape[0]
    kv_heads = keys.shape[1] // HD
    groups = queries.shape[1] // keys.shape[1]
    start = lax.axis_index("blk") * rows
    window = HOPS * rows
    blocks = [(keys, values)]
    current = (keys, values)
    for hop in range(1, HOPS + 1):
        current = shifted((current[0], current[1]), "blk", 1)
        blocks.append(current)
    query_four = queries.reshape(rows, kv_heads, groups, HD)
    q_pos = start + jnp.arange(rows, dtype=jnp.int32)
    half = kv_heads // 2
    outputs = []
    for lower in (0, half):
        query_part = query_four[:, lower : lower + half]
        score_list = []
        value_list = []
        for hop in range(HOPS, -1, -1):
            key_block, value_block = blocks[hop]
            key_part = key_block.reshape(rows, kv_heads, HD)[:, lower : lower + half]
            k_pos = start - hop * rows + jnp.arange(rows, dtype=jnp.int32)
            seen = doc_start[0] <= start - (hop - 1) * rows - 1
            scores = scores_if_seen(seen, query_part, key_part, doc_start, q_pos, k_pos, window)
            score_list.append(scores)
            value_list.append(value_block.reshape(rows, kv_heads, HD)[:, lower : lower + half])
        scores = jnp.concatenate(score_list, axis=-1)
        value_all = jnp.concatenate(value_list, axis=0)
        top = jnp.max(scores, axis=-1, keepdims=True)
        expo = jnp.exp(scores - top)
        total = jnp.sum(expo, axis=-1)
        weights = expo.astype(jnp.bfloat16)
        mixed = jnp.einsum("grqk,kgd->qgrd", weights, value_all, preferred_element_type=jnp.float32)
        mixed = mixed / jnp.transpose(total, (2, 0, 1))[..., None]
        outputs.append(mixed)
    joined = jnp.concatenate(outputs, axis=1)
    return joined.reshape(rows, kv_heads * groups * HD).astype(jnp.bfloat16)


def solution(mesh):
    return jax.shard_map(
        per_device,
        mesh=mesh,
        in_specs=(P("blk", None), P("blk", None), P("blk", None), P("blk")),
        out_specs=P("blk", None),
        check_vma=False,
    )
```

profile of v0, /device:TPU:4, one launch (start us, length us, event | category | flops | bytes accessed | tf_op | source)
XLA Modules:
  0.0 69.8 jit_solution(3950862972839517807)
XLA Ops:
  0.0 2.0 %collective-permute-start.4 = (bf16[64,2048]{1,0:T(8,128)(2,1)}, bf16[64,2048]{1,0:T(8,128)(2,1)S(1)}, u32[]{:S(2)}, u32[]{:S(2)}) collective-permute-start(bf16[64,2048]{1,0:T(8,128)(2,1)} %param.25), channel_id=1, source_target_pairs={{0,1},{1,2},{2,3},{3,4},{4,5},{5,6},{6,7},{7,8},{8,9},{9,10},{10,1... | collective-permute-start | bytes 786440 | tf_op jit(solution)/shard_map/ppermute | solution.py:18
  2.1 3.9 %collective-permute-start = (bf16[64,2048]{1,0:T(8,128)(2,1)}, bf16[64,2048]{1,0:T(8,128)(2,1)S(1)}, u32[]{:S(2)}, u32[]{:S(2)}) collective-permute-start(bf16[64,2048]{1,0:T(8,128)(2,1)} %param.26), channel_id=1, source_target_pairs={{0,1},{1,2},{2,3},{3,4},{4,5},{5,6},{6,7},{7,8},{8,9},{9,10},{10,1... | collective-permute-start | bytes 786440 | tf_op jit(solution)/shard_map/ppermute | solution.py:18
  6.0 1.4 %reshape.111 = bf16[64,8,2,256]{3,2,1,0:T(2,128)(2,1)S(1)} reshape(bf16[64,4096]{1,0:T(8,128)(2,1)} %param.24) | data formatting | bytes 1048576 | tf_op jit(solution)/shard_map/reshape | solution.py:51
  9.3 8.3 %collective-permute-done.4 = bf16[64,2048]{1,0:T(8,128)(2,1)S(1)} collective-permute-done((bf16[64,2048]{1,0:T(8,128)(2,1)}, bf16[64,2048]{1,0:T(8,128)(2,1)S(1)}, u32[]{:S(2)}, u32[]{:S(2)}) %collective-permute-start.4) | collective-permute-done | bytes 262176 | tf_op jit(solution)/shard_map/ppermute | solution.py:18
  17.6 1.9 %collective-permute-start.5 = (bf16[64,2048]{1,0:T(8,128)(2,1)S(1)}, bf16[64,2048]{1,0:T(8,128)(2,1)S(1)}, u32[]{:S(2)}, u32[]{:S(2)}) collective-permute-start(bf16[64,2048]{1,0:T(8,128)(2,1)S(1)} %collective-permute-done.4), channel_id=1, source_target_pairs={{0,1},{1,2},{2,3},{3,4},{4,5},{5,6},{6,7},{7,8},{8,9},{9,10},{10,1... | collective-permute-start | bytes 786440 | tf_op jit(solution)/shard_map/ppermute | solution.py:18
  20.5 1.9 %collective-permute-start.1 = (bf16[64,2048]{1,0:T(8,128)(2,1)S(1)}, bf16[64,2048]{1,0:T(8,128)(2,1)S(1)}, u32[]{:S(2)}, u32[]{:S(2)}) collective-permute-start(bf16[64,2048]{1,0:T(8,128)(2,1)S(1)} %collective-permute-done), channel_id=1, source_target_pairs={{0,1},{1,2},{2,3},{3,4},{4,5},{5,6},{6,7},{7,8},{8,9},{9,10},{10,1... | collective-permute-start | bytes 786440 | tf_op jit(solution)/shard_map/ppermute | solution.py:18
  23.0 6.6 %collective-permute-done.5 = bf16[64,2048]{1,0:T(8,128)(2,1)S(1)} collective-permute-done((bf16[64,2048]{1,0:T(8,128)(2,1)S(1)}, bf16[64,2048]{1,0:T(8,128)(2,1)S(1)}, u32[]{:S(2)}, u32[]{:S(2)}) %collective-permute-start.5) | collective-permute-done | bytes 262176 | tf_op jit(solution)/shard_map/ppermute | solution.py:18
  29.5 1.9 %collective-permute-start.6 = (bf16[64,2048]{1,0:T(8,128)(2,1)S(1)}, bf16[64,2048]{1,0:T(8,128)(2,1)S(1)}, u32[]{:S(2)}, u32[]{:S(2)}) collective-permute-start(bf16[64,2048]{1,0:T(8,128)(2,1)S(1)} %collective-permute-done.5), channel_id=1, source_target_pairs={{0,1},{1,2},{2,3},{3,4},{4,5},{5,6},{6,7},{7,8},{8,9},{9,10},{10,1... | collective-permute-start | bytes 786440 | tf_op jit(solution)/shard_map/ppermute | solution.py:18
  31.8 1.4 %conditional.14 = (f32[4,2,64,64]{2,3,1,0:T(8,128)S(1)}) conditional(s32[]{:T(128)} %convert_element_type.34, () %tuple.73, (s32[64]{0:T(128)S(1)}, s32[64]{0:T(128)S(1)}, bf16[64,8,256]{2,1,0:T(8,128)(2,1)S(1)}, bf16[64,4,2,256]{3,2,1,0:T(2,128)(2,1)}) %tuple.146), branch_computations={%region_8.9_spmd, %region_9.10_spmd} | conditional | flops 16867328 | bytes 1061384 | solution.py:37
  31.9 1.2 %fusion.21 = f32[4,2,64,64]{2,3,1,0:T(8,128)S(1)} fusion(bf16[64,4,2,256]{3,2,1,0:T(2,128)(2,1)} %get-tuple-element.214, bf16[64,8,256]{2,0,1:T(8,128)(2,1)S(1)} %copy.20, pred[64,64]{0,1:T(8,128)(4,1)S(1)} %fusion.24), kind=kOutput, calls=%fused_computation.34 | convolution fusion | flops 16842752 | bytes 532480 | tf_op jit(solution)/shard_map/cond/branch_1_fun/qgrd,kgd->grqk/dot_general | solution.py:23
  33.6 1.9 %collective-permute-start.2 = (bf16[64,2048]{1,0:T(8,128)(2,1)S(1)}, bf16[64,2048]{1,0:T(8,128)(2,1)}, u32[]{:S(2)}, u32[]{:S(2)}) collective-permute-start(bf16[64,2048]{1,0:T(8,128)(2,1)S(1)} %collective-permute-done.1), channel_id=1, source_target_pairs={{0,1},{1,2},{2,3},{3,4},{4,5},{5,6},{6,7},{7,8},{8,9},{9,10},{10,1... | collective-permute-start | bytes 786440 | tf_op jit(solution)/shard_map/ppermute | solution.py:18
  36.4 1.4 %conditional.13 = (f32[4,2,64,64]{2,3,1,0:T(8,128)S(1)}) conditional(s32[]{:T(128)} %convert_element_type.33, () %tuple.71, (s32[64]{0:T(128)S(1)}, s32[64]{0:T(128)S(1)}, s32[64]{0:T(128)S(1)}, bf16[64,8,256]{2,1,0:T(8,128)(2,1)S(1)}, bf16[64,4,2,256]{3,2,1,0:T(2,128)(2,1)}) %tuple.148), branch_computations={%region_6.7_spmd, %region_7.8_spmd} | conditional | flops 16867328 | bytes 1061640 | solution.py:37
  36.6 1.2 %fusion.16 = f32[4,2,64,64]{2,3,1,0:T(8,128)S(1)} fusion(bf16[64,4,2,256]{3,2,1,0:T(2,128)(2,1)} %get-tuple-element.210, bf16[64,8,256]{2,0,1:T(8,128)(2,1)S(1)} %copy.18, pred[64,64]{0,1:T(8,128)(4,1)S(1)} %fusion.19), kind=kOutput, calls=%fused_computation.26 | convolution fusion | flops 16842752 | bytes 532480 | tf_op jit(solution)/shard_map/cond/branch_1_fun/qgrd,kgd->grqk/dot_general | solution.py:23
  38.3 3.2 %collective-permute-done.6 = bf16[64,2048]{1,0:T(8,128)(2,1)S(1)} collective-permute-done((bf16[64,2048]{1,0:T(8,128)(2,1)S(1)}, bf16[64,2048]{1,0:T(8,128)(2,1)S(1)}, u32[]{:S(2)}, u32[]{:S(2)}) %collective-permute-start.6) | collective-permute-done | bytes 262176 | tf_op jit(solution)/shard_map/ppermute | solution.py:18
  41.4 1.9 %collective-permute-start.7 = (bf16[64,2048]{1,0:T(8,128)(2,1)S(1)}, bf16[64,2048]{1,0:T(8,128)(2,1)S(1)}, u32[]{:S(2)}, u32[]{:S(2)}) collective-permute-start(bf16[64,2048]{1,0:T(8,128)(2,1)S(1)} %collective-permute-done.6), channel_id=1, source_target_pairs={{0,1},{1,2},{2,3},{3,4},{4,5},{5,6},{6,7},{7,8},{8,9},{9,10},{10,1... | collective-permute-start | bytes 786440 | tf_op jit(solution)/shard_map/ppermute | solution.py:18
  44.2 1.4 %conditional.12 = (f32[4,2,64,64]{2,3,1,0:T(8,128)S(1)}) conditional(s32[]{:T(128)} %convert_element_type.32, () %tuple.69, (s32[64]{0:T(128)S(1)}, s32[64]{0:T(128)S(1)}, s32[64]{0:T(128)S(1)}, bf16[64,8,256]{2,1,0:T(8,128)(2,1)S(1)}, bf16[64,4,2,256]{3,2,1,0:T(2,128)(2,1)}) %tuple.156), branch_computations={%region_4.5_spmd, %region_5.6_spmd} | conditional | flops 16867328 | bytes 1061640 | solution.py:37
  44.4 1.2 %fusion.11 = f32[4,2,64,64]{2,3,1,0:T(8,128)S(1)} fusion(bf16[64,4,2,256]{3,2,1,0:T(2,128)(2,1)} %get-tuple-element.205, bf16[64,8,256]{2,0,1:T(8,128)(2,1)S(1)} %copy.16, pred[64,64]{0,1:T(8,128)(4,1)S(1)} %fusion.14), kind=kOutput, calls=%fused_computation.18 | convolution fusion | flops 16842752 | bytes 532480 | tf_op jit(solution)/shard_map/cond/branch_1_fun/qgrd,kgd->grqk/dot_general | solution.py:23
  45.6 1.9 %conditional.17 = (f32[4,2,64,64]{2,3,1,0:T(8,128)S(1)}) conditional(s32[]{:T(128)} %convert_element_type.32, () %tuple.79, (s32[64]{0:T(128)S(1)}, s32[64]{0:T(128)S(1)}, s32[64]{0:T(128)S(1)}, bf16[64,8,256]{2,1,0:T(8,128)(2,1)S(1)}, bf16[64,4,2,256]{3,2,1,0:T(2,128)(2,1)S(1)}) %tuple.157), branch_computations={%region_20.21_spmd, %region_21.22_spmd} | conditional | flops 16867328 | bytes 2110244 | solution.py:37
  48.6 1.4 %conditional.11 = (f32[4,2,64,64]{2,3,1,0:T(8,128)S(1)}) conditional(s32[]{:T(128)} %convert_element_type.31, () %tuple.67, (s32[64]{0:T(128)S(1)}, s32[64]{0:T(128)S(1)}, s32[64]{0:T(128)S(1)}, bf16[64,8,256]{2,1,0:T(8,128)(2,1)S(1)}, bf16[64,4,2,256]{3,2,1,0:T(2,128)(2,1)}) %tuple.152), branch_computations={%region_2.3_spmd, %region_3.4_spmd} | conditional | flops 16867328 | bytes 1061640 | solution.py:37
  48.8 1.2 %fusion.6 = f32[4,2,64,64]{2,3,1,0:T(8,128)S(1)} fusion(bf16[64,4,2,256]{3,2,1,0:T(2,128)(2,1)} %get-tuple-element.200, bf16[64,8,256]{2,0,1:T(8,128)(2,1)S(1)} %copy.14, pred[64,64]{0,1:T(8,128)(4,1)S(1)} %fusion.9), kind=kOutput, calls=%fused_computation.10 | convolution fusion | flops 16842752 | bytes 532480 | tf_op jit(solution)/shard_map/cond/branch_1_fun/qgrd,kgd->grqk/dot_general | solution.py:23
  50.0 1.4 %conditional.16 = (f32[4,2,64,64]{2,3,1,0:T(8,128)S(1)}) conditional(s32[]{:T(128)} %convert_element_type.31, () %tuple.77, (s32[64]{0:T(128)S(1)}, s32[64]{0:T(128)S(1)}, s32[64]{0:T(128)S(1)}, bf16[64,8,256]{2,1,0:T(8,128)(2,1)S(1)}, bf16[64,4,2,256]{3,2,1,0:T(2,128)(2,1)}) %tuple.153), branch_computations={%region_18.19_spmd, %region_19.20_spmd} | conditional | flops 16867328 | bytes 1061640 | solution.py:37
  50.2 1.2 %fusion.31 = f32[4,2,64,64]{2,3,1,0:T(8,128)S(1)} fusion(bf16[64,4,2,256]{3,2,1,0:T(2,128)(2,1)} %get-tuple-element.224, bf16[64,8,256]{2,0,1:T(8,128)(2,1)S(1)} %copy.30, pred[64,64]{0,1:T(8,128)(4,1)S(1)} %fusion.34), kind=kOutput, calls=%fused_computation.50 | convolution fusion | flops 16842752 | bytes 532480 | tf_op jit(solution)/shard_map/cond/branch_1_fun/qgrd,kgd->grqk/dot_general | solution.py:23
  51.4 1.9 %collective-permute-start.3 = (bf16[64,2048]{1,0:T(8,128)(2,1)}, bf16[64,2048]{1,0:T(8,128)(2,1)}, u32[]{:S(2)}, u32[]{:S(2)}) collective-permute-start(bf16[64,2048]{1,0:T(8,128)(2,1)} %collective-permute-done.2), channel_id=1, source_target_pairs={{0,1},{1,2},{2,3},{3,4},{4,5},{5,6},{6,7},{7,8},{8,9},{9,10},{10,1... | collective-permute-start | bytes 786440 | tf_op jit(solution)/shard_map/ppermute | solution.py:18
  54.4 9.2 %collective-permute-done.3 = bf16[64,2048]{1,0:T(8,128)(2,1)} collective-permute-done((bf16[64,2048]{1,0:T(8,128)(2,1)}, bf16[64,2048]{1,0:T(8,128)(2,1)}, u32[]{:S(2)}, u32[]{:S(2)}) %collective-permute-start.3) | collective-permute-done | bytes 262176 | tf_op jit(solution)/shard_map/ppermute | solution.py:18
  (111 shorter events, 17.4 us)
Async XLA Ops:
  0.0 8.5 %copy-start.11 = (bf16[64,2048]{1,0:T(8,128)(2,1)S(1)}, bf16[64,2048]{1,0:T(8,128)(2,1)}, u32[]{:S(2)}) copy-start(bf16[64,2048]{1,0:T(8,128)(2,1)} %param.26) | copy-start | bytes 786436
  0.0 17.6 %collective-permute-start.4 = (bf16[64,2048]{1,0:T(8,128)(2,1)}, bf16[64,2048]{1,0:T(8,128)(2,1)S(1)}, u32[]{:S(2)}, u32[]{:S(2)}) collective-permute-start(bf16[64,2048]{1,0:T(8,128)(2,1)} %param.25), channel_id=1, source_target_pairs={{0,1},{1,2},{2,3},{3,4},{4,5},{5,6},{6,7},{7,8},{8,9},{9,10},{10,1... | collective-permute-start | bytes 786440 | tf_op jit(solution)/shard_map/ppermute | solution.py:18
  2.1 18.4 %collective-permute-start = (bf16[64,2048]{1,0:T(8,128)(2,1)}, bf16[64,2048]{1,0:T(8,128)(2,1)S(1)}, u32[]{:S(2)}, u32[]{:S(2)}) collective-permute-start(bf16[64,2048]{1,0:T(8,128)(2,1)} %param.26), channel_id=1, source_target_pairs={{0,1},{1,2},{2,3},{3,4},{4,5},{5,6},{6,7},{7,8},{8,9},{9,10},{10,1... | collective-permute-start | bytes 786440 | tf_op jit(solution)/shard_map/ppermute | solution.py:18
  7.4 24.1 %copy-start.15 = (s32[64]{0:T(128)S(1)}, s32[64]{0:T(128)}, u32[]{:S(2)}) copy-start(s32[64]{0:T(128)} %param.27) | copy-start | bytes 772
  7.4 24.2 %copy-start.12 = (bf16[64,2048]{1,0:T(8,128)(2,1)S(1)}, bf16[64,2048]{1,0:T(8,128)(2,1)}, u32[]{:S(2)}) copy-start(bf16[64,2048]{1,0:T(8,128)(2,1)} %param.25) | copy-start | bytes 786436
  8.5 37.1 %copy-start.13 = (bf16[64,4,2,256]{3,2,1,0:T(2,128)(2,1)}, bf16[64,4,2,256]{3,2,1,0:T(2,128)(2,1)S(1)}, u32[]{:S(2)}) copy-start(bf16[64,4,2,256]{3,2,1,0:T(2,128)(2,1)S(1)} %get-tuple-element.240) | copy-start | bytes 786436
  17.6 11.9 %collective-permute-start.5 = (bf16[64,2048]{1,0:T(8,128)(2,1)S(1)}, bf16[64,2048]{1,0:T(8,128)(2,1)S(1)}, u32[]{:S(2)}, u32[]{:S(2)}) collective-permute-start(bf16[64,2048]{1,0:T(8,128)(2,1)S(1)} %collective-permute-done.4), channel_id=1, source_target_pairs={{0,1},{1,2},{2,3},{3,4},{4,5},{5,6},{6,7},{7,8},{8,9},{9,10},{10,1... | collective-permute-start | bytes 786440 | tf_op jit(solution)/shard_map/ppermute | solution.py:18
  20.5 13.1 %collective-permute-start.1 = (bf16[64,2048]{1,0:T(8,128)(2,1)S(1)}, bf16[64,2048]{1,0:T(8,128)(2,1)S(1)}, u32[]{:S(2)}, u32[]{:S(2)}) collective-permute-start(bf16[64,2048]{1,0:T(8,128)(2,1)S(1)} %collective-permute-done), channel_id=1, source_target_pairs={{0,1},{1,2},{2,3},{3,4},{4,5},{5,6},{6,7},{7,8},{8,9},{9,10},{10,1... | collective-permute-start | bytes 786440 | tf_op jit(solution)/shard_map/ppermute | solution.py:18
  29.5 11.9 %collective-permute-start.6 = (bf16[64,2048]{1,0:T(8,128)(2,1)S(1)}, bf16[64,2048]{1,0:T(8,128)(2,1)S(1)}, u32[]{:S(2)}, u32[]{:S(2)}) collective-permute-start(bf16[64,2048]{1,0:T(8,128)(2,1)S(1)} %collective-permute-done.5), channel_id=1, source_target_pairs={{0,1},{1,2},{2,3},{3,4},{4,5},{5,6},{6,7},{7,8},{8,9},{9,10},{10,1... | collective-permute-start | bytes 786440 | tf_op jit(solution)/shard_map/ppermute | solution.py:18
  33.6 14.0 %collective-permute-start.2 = (bf16[64,2048]{1,0:T(8,128)(2,1)S(1)}, bf16[64,2048]{1,0:T(8,128)(2,1)}, u32[]{:S(2)}, u32[]{:S(2)}) collective-permute-start(bf16[64,2048]{1,0:T(8,128)(2,1)S(1)} %collective-permute-done.1), channel_id=1, source_target_pairs={{0,1},{1,2},{2,3},{3,4},{4,5},{5,6},{6,7},{7,8},{8,9},{9,10},{10,1... | collective-permute-start | bytes 786440 | tf_op jit(solution)/shard_map/ppermute | solution.py:18
  37.8 6.5 %copy-start.16 = (s32[64]{0:T(128)S(1)}, s32[64]{0:T(128)}, u32[]{:S(2)}) copy-start(s32[64]{0:T(128)} %iota_add_fusion.1) | copy-start | bytes 772
  41.4 12.7 %collective-permute-start.7 = (bf16[64,2048]{1,0:T(8,128)(2,1)S(1)}, bf16[64,2048]{1,0:T(8,128)(2,1)S(1)}, u32[]{:S(2)}, u32[]{:S(2)}) collective-permute-start(bf16[64,2048]{1,0:T(8,128)(2,1)S(1)} %collective-permute-done.6), channel_id=1, source_target_pairs={{0,1},{1,2},{2,3},{3,4},{4,5},{5,6},{6,7},{7,8},{8,9},{9,10},{10,1... | collective-permute-start | bytes 786440 | tf_op jit(solution)/shard_map/ppermute | solution.py:18
  50.0 4.2 %copy-start = (f32[4,2,64,64]{2,3,1,0:T(8,128)}, f32[4,2,64,64]{2,3,1,0:T(8,128)S(1)}, u32[]{:S(2)}) copy-start(f32[4,2,64,64]{2,3,1,0:T(8,128)S(1)} %get-tuple-element.276) | copy-start | bytes 393220
  51.4 2.9 %copy-start.2 = (f32[4,2,64,64]{2,3,1,0:T(8,128)}, f32[4,2,64,64]{2,3,1,0:T(8,128)S(1)}, u32[]{:S(2)}) copy-start(f32[4,2,64,64]{2,3,1,0:T(8,128)S(1)} %get-tuple-element.281) | copy-start | bytes 393220
  51.4 12.2 %collective-permute-start.3 = (bf16[64,2048]{1,0:T(8,128)(2,1)}, bf16[64,2048]{1,0:T(8,128)(2,1)}, u32[]{:S(2)}, u32[]{:S(2)}) collective-permute-start(bf16[64,2048]{1,0:T(8,128)(2,1)} %collective-permute-done.2), channel_id=1, source_target_pairs={{0,1},{1,2},{2,3},{3,4},{4,5},{5,6},{6,7},{7,8},{8,9},{9,10},{10,1... | collective-permute-start | bytes 786440 | tf_op jit(solution)/shard_map/ppermute | solution.py:18
  54.3 10.4 %copy-start.1 = (f32[4,2,64,64]{2,3,1,0:T(8,128)S(1)}, f32[4,2,64,64]{2,3,1,0:T(8,128)}, u32[]{:S(2)}) copy-start(f32[4,2,64,64]{2,3,1,0:T(8,128)} %copy-done) | copy-start | bytes 393220
  54.3 10.4 %copy-start.3 = (f32[4,2,64,64]{2,3,1,0:T(8,128)S(1)}, f32[4,2,64,64]{2,3,1,0:T(8,128)}, u32[]{:S(2)}) copy-start(f32[4,2,64,64]{2,3,1,0:T(8,128)} %copy-done.2) | copy-start | bytes 393220
  64.9 0.9 %copy-start.10 = (bf16[64,4,256]{2,1,0:T(4,128)(2,1)S(1)}, bf16[64,4,256]{2,1,0:T(4,128)(2,1)}, u32[]{:S(2)}) copy-start(bf16[64,4,256]{2,1,0:T(4,128)(2,1)} %get-tuple-element.257) | copy-start | bytes 393220
  64.9 1.0 %copy-start.8 = (bf16[64,4,256]{2,1,0:T(4,128)(2,1)S(1)}, bf16[64,4,256]{2,1,0:T(4,128)(2,1)}, u32[]{:S(2)}) copy-start(bf16[64,4,256]{2,1,0:T(4,128)(2,1)} %get-tuple-element.255) | copy-start | bytes 393220
  64.9 1.0 %copy-start.6 = (bf16[64,4,256]{2,1,0:T(4,128)(2,1)S(1)}, bf16[64,4,256]{2,1,0:T(4,128)(2,1)}, u32[]{:S(2)}) copy-start(bf16[64,4,256]{2,1,0:T(4,128)(2,1)} %get-tuple-element.253) | copy-start | bytes 393220
  65.0 1.0 %copy-start.4 = (bf16[64,4,256]{2,1,0:T(4,128)(2,1)S(1)}, bf16[64,4,256]{2,1,0:T(4,128)(2,1)}, u32[]{:S(2)}) copy-start(bf16[64,4,256]{2,1,0:T(4,128)(2,1)} %get-tuple-element.251) | copy-start | bytes 393220
  66.5 0.9 %copy-start.9 = (bf16[64,4,256]{2,1,0:T(4,128)(2,1)S(1)}, bf16[64,4,256]{2,1,0:T(4,128)(2,1)}, u32[]{:S(2)}) copy-start(bf16[64,4,256]{2,1,0:T(4,128)(2,1)} %get-tuple-element.258) | copy-start | bytes 393220
  66.5 1.0 %copy-start.7 = (bf16[64,4,256]{2,1,0:T(4,128)(2,1)S(1)}, bf16[64,4,256]{2,1,0:T(4,128)(2,1)}, u32[]{:S(2)}) copy-start(bf16[64,4,256]{2,1,0:T(4,128)(2,1)} %get-tuple-element.256) | copy-start | bytes 393220
  66.5 1.0 %copy-start.5 = (bf16[64,4,256]{2,1,0:T(4,128)(2,1)S(1)}, bf16[64,4,256]{2,1,0:T(4,128)(2,1)}, u32[]{:S(2)}) copy-start(bf16[64,4,256]{2,1,0:T(4,128)(2,1)} %get-tuple-element.254) | copy-start | bytes 393220
  (1 other events, 0.7 us)
where the time goes:
time: 70.6 us; the launch traced here: 69.8 us
  waiting for transfers between devices  28.2 us (40%)
  starting transfers between devices  17.4 us (25%)
  local copies, waits for them, and re-layouts  12.4 us (18%)
  matrix products  8.58 us (12%)
  other arithmetic  2.14 us (3%)
    ppermute x8, waiting for transfers between devices, shifted(): return lax.ppermute(block, axis, route)  28.2 us
    ppermute x8, starting transfers between devices, shifted(): return lax.ppermute(block, axis, route)  17.4 us
    dot_general x8, matrix products, masked_scores(): jnp.einsum('qgrd,kgd->grqk', query_part, key_part, preferred_element_type...  7.74 us
    unnamed x49, local copies, waits for them, and re-layouts  3.93 us
    slice x5, local copies, waits for them, and re-layouts, per_device(): value_block.reshape(rows, kv_heads, HD)[:, lower:lower + half]  3.24 us
    reshape x1, local copies, waits for them, and re-layouts, per_device(): query_four = queries.reshape(rows, kv_heads, groups, HD)  1.42 us
  transfers between devices with their start and end apart: 8, of which 5 were waited for; matrix products, arithmetic and copies ran while one was open for 24% of the time, Pallas kernels for 0%

commit v1 on v0

v1 whole, which is shorter than its diff:
```python
import functools

import jax
import jax.numpy as jnp
from jax import lax
from jax.experimental import pallas as pl
from jax.experimental.pallas import tpu as pltpu
from jax.sharding import PartitionSpec as P

HD = 256
HOPS = 4
MESH = pl.DeviceIdType.MESH


def kernel(devices, rows, kv_heads, groups, q_hbm, k_hbm, v_hbm, starts_hbm, out_ref,
           q_ref, k_ref, v_ref, starts_ref, bias_ref, load_sem, own_send, near_recv, fwd_send, far_recv,
           a_send, a_recv, b_send, b_recv, misc_sem):
    me = lax.axis_index("blk")
    core = lax.rem(me, 2)
    ahead = lax.rem(me + 2, devices)
    behind = lax.rem(me + devices - 2, devices)
    partner = me + 1 - 2 * core
    span = (HOPS + 1) * rows

    barrier = pltpu.get_barrier_semaphore()
    for peer in (behind, partner):
        pl.semaphore_signal(barrier, inc=1, device_id=(peer,), device_id_type=MESH)

    pairs = ((k_hbm, k_ref), (v_hbm, v_ref))

    def columns(h):
        return pl.ds(pl.multiple_of(h * HD, HD), HD)

    def slot(index):
        return pl.ds(index * rows, rows)

    def load(h, t):
        source, target = pairs[t]
        return pltpu.make_async_copy(
            source.at[:, columns(h)], target.at[slot(HOPS), columns(h)], load_sem.at[2 * h + t])

    def remote(h, t, source_rows, target_rows, send, recv, device):
        ref = pairs[t][1]
        return pltpu.make_async_remote_copy(
            src_ref=ref.at[source_rows, columns(h)], dst_ref=ref.at[target_rows, columns(h)],
            send_sem=send.at[2 * h + t], recv_sem=recv.at[2 * h + t],
            device_id=(device,), device_id_type=MESH)

    def near(h, t):
        return remote(h, t, slot(4), slot(2), own_send, near_recv, ahead)

    def far(h, t):
        return remote(h, t, slot(2), slot(0), fwd_send, far_recv, ahead)

    def side_a(h, t):
        first = pl.multiple_of((4 - 2 * core) * rows, rows)
        return remote(h, t, pl.ds(first, rows), slot(3), a_send, a_recv, partner)

    def side_b(h, t):
        first = pl.multiple_of((2 - 2 * core) * rows, rows)
        return remote(h, t, pl.ds(first, rows), slot(1), b_send, b_recv, partner)

    starts_copy = pltpu.make_async_copy(starts_hbm, starts_ref, misc_sem.at[0])
    q_copy = pltpu.make_async_copy(q_hbm, q_ref, misc_sem.at[1])

    def start_load(h, carry):
        for t in range(2):
            load(h, t).start()
        return carry

    lax.fori_loop(0, kv_heads, start_load, 0)
    starts_copy.start()
    q_copy.start()
    pl.semaphore_wait(barrier, 2)

    def start_own(h, carry):
        for t in range(2):
            load(h, t).wait()
            near(h, t).start()

            @pl.when(core == 0)
            def _():
                side_a(h, t).start()
        return carry

    lax.fori_loop(0, kv_heads, start_own, 0)

    starts_copy.wait()
    row = lax.broadcasted_iota(jnp.int32, (rows, rows), 0)
    column = lax.broadcasted_iota(jnp.int32, (rows, rows), 1)
    spread = jnp.broadcast_to(starts_ref[...].astype(jnp.float32), (rows, rows))
    first = jnp.sum(jnp.where(row == column, spread, 0.0), axis=1, keepdims=True)
    start = me * rows
    q_pos = start + lax.broadcasted_iota(jnp.int32, (rows, span), 0)
    k_pos = start - HOPS * rows + lax.broadcasted_iota(jnp.int32, (rows, span), 1)
    allowed = (k_pos <= q_pos) & (q_pos - k_pos < HOPS * rows) & (k_pos.astype(jnp.float32) >= first)
    bias_ref[...] = jnp.where(allowed, 0.0, -1e30)
    q_copy.wait()

    def relay(h, carry):
        for t in range(2):
            near(h, t).wait_recv()
            far(h, t).start()

            @pl.when(core == 0)
            def _():
                side_b(h, t).start()

            @pl.when(core == 1)
            def _():
                side_a(h, t).start()
        return carry

    lax.fori_loop(0, kv_heads, relay, 0)

    def attend(h, carry):
        for t in range(2):
            far(h, t).wait_recv()

            @pl.when(core == 1)
            def _():
                side_b(h, t).start()
        for t in range(2):
            side_a(h, t).wait_recv()
            side_b(h, t).wait_recv()
        key = k_ref[:, columns(h)]
        value = v_ref[:, columns(h)]
        for g in range(groups):
            head = pl.ds(pl.multiple_of((h * groups + g) * HD, HD), HD)
            scores = lax.dot_general(
                q_ref[:, head], key, (((1,), (1,)), ((), ())), preferred_element_type=jnp.float32)
            scores = scores * 0.0625 + bias_ref[...]
            top = jnp.max(scores, axis=1, keepdims=True)
            expo = jnp.exp(scores - top)
            total = jnp.sum(expo, axis=1, keepdims=True)
            mixed = jnp.dot(expo.astype(jnp.bfloat16), value, preferred_element_type=jnp.float32)
            out_ref[:, head] = (mixed / total).astype(out_ref.dtype)
        return carry

    lax.fori_loop(0, kv_heads, attend, 0)

    def drain(h, carry):
        for t in range(2):
            near(h, t).wait_send()
            far(h, t).wait_send()
            side_a(h, t).wait_send()
            side_b(h, t).wait_send()
        return carry

    lax.fori_loop(0, kv_heads, drain, 0)


def per_device(devices, queries, keys, values, doc_start):
    rows = queries.shape[0]
    kv_heads = keys.shape[1] // HD
    groups = queries.shape[1] // keys.shape[1]
    span = (HOPS + 1) * rows
    copies = pltpu.SemaphoreType.DMA((2 * kv_heads,))
    return pl.pallas_call(
        functools.partial(kernel, devices, rows, kv_heads, groups),
        out_shape=jax.ShapeDtypeStruct(queries.shape, jnp.bfloat16),
        in_specs=[pl.BlockSpec(memory_space=pl.ANY)] * 4,
        out_specs=pl.BlockSpec(memory_space=pltpu.VMEM),
        scratch_shapes=[
            pltpu.VMEM(queries.shape, jnp.bfloat16),
            pltpu.VMEM((span, keys.shape[1]), jnp.bfloat16),
            pltpu.VMEM((span, keys.shape[1]), jnp.bfloat16),
            pltpu.VMEM((1, rows), jnp.int32),
            pltpu.VMEM((rows, span), jnp.float32),
            copies, copies, copies, copies, copies, copies, copies, copies, copies,
            pltpu.SemaphoreType.DMA((2,)),
        ],
        compiler_params=pltpu.CompilerParams(collective_id=0, has_side_effects=True),
    )(queries, keys, values, doc_start.reshape(1, rows))


def solution(mesh):
    return jax.shard_map(
        functools.partial(per_device, mesh.shape["blk"]),
        mesh=mesh,
        in_specs=(P("blk", None), P("blk", None), P("blk", None), P("blk")),
        out_specs=P("blk", None),
        check_vma=False,
    )
```

time: 70.6 us -> 44 us (0.62)
  the two profiles are of different devices: /device:TPU:4 before, /device:TPU:1 now
where the time goes in v1:
time: 44 us; the launch traced here: 43.8 us
  Pallas kernels  42 us (95%)
  local copies, waits for them, and re-layouts  1.87 us (4%)
    pallas_call x1, Pallas kernels, per_device(): pl.pallas_call(functools.partial(kernel, devices, rows, kv_heads, groups)...  42 us
    unnamed x1, local copies, waits for them, and re-layouts  1.87 us

profile of v1, /device:TPU:1, one launch (start us, length us, event | category | flops | bytes accessed | tf_op | source)
XLA Modules:
  0.0 43.8 jit_solution(17749753105218183016)
XLA Ops:
  0.0 42.0 %shard_map.46 = bf16[64,4096]{1,0:T(8,128)(2,1)} custom-call(bf16[64,4096]{1,0:T(8,128)(2,1)} %q_hbm.1, bf16[64,2048]{1,0:T(8,128)(2,1)} %k_hbm.1, bf16[64,2048]{1,0:T(8,128)(2,1)} %v_hbm.1, s32[1,64]{1,0:T(1,128)} %bitcast.1), custom_call_target="tpu_custom_call" | custom-call | tf_op jit(solution)/shard_map/pallas_call | solution.py:159
  42.0 1.9 %copy.6 = bf16[64,4096]{1,0:T(8,128)(2,1)} copy(bf16[64,4096]{1,0:T(8,128)(2,1)} %shard_map.46) | data formatting | bytes 1048576

commit v2 on v1

v2 whole, which is shorter than its diff:
```python
import functools

import jax
import jax.numpy as jnp
from jax import lax
from jax.experimental import pallas as pl
from jax.experimental.pallas import tpu as pltpu
from jax.sharding import PartitionSpec as P

HD = 256
HOPS = 4
DEPTH = 16
MESH = pl.DeviceIdType.MESH


def kernel(devices, rows, kv_heads, groups, q_hbm, k_hbm, v_hbm, starts_hbm, out_ref,
           q_ref, k_ref, v_ref, k_pass, v_pass, starts_ref, bias_ref, load_sem, own_send, near_recv,
           fwd_send, far_recv, a_send, a_recv, b_send, b_recv, pass_send, pass_recv, misc_sem):
    me = lax.axis_index("blk")
    core = lax.rem(me, 2)
    chip = lax.div(me, 2)
    chips = devices // 2
    depth = lax.rem(chip, DEPTH)
    ahead = lax.rem(me + 2, devices)
    behind = lax.rem(me + devices - 2, devices)
    partner = me + 1 - 2 * core
    span = (HOPS + 1) * rows

    has_ahead = chip < chips - 1
    has_near = chip >= 1
    has_far = chip >= 2
    inner = chip < chips - DEPTH
    detour_first = inner & (depth == DEPTH - 2)
    detour_middle = inner & (depth == DEPTH // 2 - 1)
    detour_last = (depth == 0) & (chip > 0)
    short = inner & (depth == DEPTH - 1)
    to_middle = lax.rem(me + devices - DEPTH + 2, devices)
    to_last = lax.rem(me + DEPTH + 2, devices)

    @pl.when(chip < 2)
    def _():
        for ref in (k_ref, v_ref):
            ref[pl.ds(0, HOPS * rows), :] = jnp.zeros((HOPS * rows, ref.shape[1]), ref.dtype)

    barrier = pltpu.get_barrier_semaphore()

    def greet(peer):
        pl.semaphore_signal(barrier, inc=1, device_id=(peer,), device_id_type=MESH)

    greet(partner)

    @pl.when(has_near)
    def _():
        greet(behind)

    @pl.when(detour_middle)
    def _():
        greet(lax.rem(me + DEPTH - 2, devices))

    @pl.when(detour_last)
    def _():
        greet(lax.rem(me + devices - DEPTH - 2, devices))

    pairs = ((k_hbm, k_ref, k_pass), (v_hbm, v_ref, v_pass))

    def columns(h):
        return pl.ds(pl.multiple_of(h * HD, HD), HD)

    def slot(index):
        return pl.ds(index * rows, rows)

    def load(h, t):
        source, target, _ = pairs[t]
        return pltpu.make_async_copy(
            source.at[:, columns(h)], target.at[slot(HOPS), columns(h)], load_sem.at[2 * h + t])

    def remote(source, target, send, recv, device):
        return pltpu.make_async_remote_copy(
            src_ref=source, dst_ref=target, send_sem=send, recv_sem=recv,
            device_id=(device,), device_id_type=MESH)

    def between(h, t, source_rows, target_rows, send, recv, device):
        ref = pairs[t][1]
        return remote(ref.at[source_rows, columns(h)], ref.at[target_rows, columns(h)],
                      send.at[2 * h + t], recv.at[2 * h + t], device)

    def near(h, t):
        return between(h, t, slot(4), slot(2), own_send, near_recv, ahead)

    def far(h, t):
        return between(h, t, slot(2), slot(0), fwd_send, far_recv, ahead)

    def side_a(h, t):
        first = pl.multiple_of((4 - 2 * core) * rows, rows)
        return between(h, t, pl.ds(first, rows), slot(3), a_send, a_recv, partner)

    def side_b(h, t):
        first = pl.multiple_of((2 - 2 * core) * rows, rows)
        return between(h, t, pl.ds(first, rows), slot(1), b_send, b_recv, partner)

    def pass_in(j, t):
        _, ref, buffer = pairs[t]
        return remote(ref.at[slot(4), columns(2 * j + 1)], buffer.at[:, columns(j)],
                      pass_send.at[2 * j + t], pass_recv.at[2 * j + t], to_middle)

    def pass_out(j, t):
        _, ref, buffer = pairs[t]
        return remote(buffer.at[:, columns(j)], ref.at[slot(0), columns(2 * j + 1)],
                      pass_send.at[2 * j + t], far_recv.at[2 * (2 * j + 1) + t], to_last)

    starts_copy = pltpu.make_async_copy(starts_hbm, starts_ref, misc_sem.at[0])
    q_copy = pltpu.make_async_copy(q_hbm, q_ref, misc_sem.at[1])

    def start_load(h, carry):
        for t in range(2):
            load(h, t).start()
        return carry

    lax.fori_loop(0, kv_heads, start_load, 0)
    starts_copy.start()
    q_copy.start()

    awaited = 1 + has_ahead.astype(jnp.int32) + (detour_first | detour_middle).astype(jnp.int32)
    pl.semaphore_wait(barrier, awaited)

    def start_own(h, carry):
        for t in range(2):
            load(h, t).wait()

            @pl.when(has_ahead)
            def _():
                near(h, t).start()

            @pl.when(detour_first & (lax.rem(h, 2) == 1))
            def _():
                pass_in(lax.div(h, 2), t).start()

            @pl.when(core == 0)
            def _():
                side_a(h, t).start()
        return carry

    lax.fori_loop(0, kv_heads, start_own, 0)

    starts_copy.wait()
    row = lax.broadcasted_iota(jnp.int32, (rows, rows), 0)
    column = lax.broadcasted_iota(jnp.int32, (rows, rows), 1)
    spread = jnp.broadcast_to(starts_ref[...].astype(jnp.float32), (rows, rows))
    first = jnp.sum(jnp.where(row == column, spread, 0.0), axis=1, keepdims=True)
    start = me * rows
    q_pos = start + lax.broadcasted_iota(jnp.int32, (rows, span), 0)
    k_pos = start - HOPS * rows + lax.broadcasted_iota(jnp.int32, (rows, span), 1)
    allowed = (k_pos <= q_pos) & (q_pos - k_pos < HOPS * rows) & (k_pos.astype(jnp.float32) >= first)
    bias_ref[...] = jnp.where(allowed, 0.0, -1e30)
    q_copy.wait()

    def sends_far(h):
        return has_near & has_ahead & jnp.logical_not(short & (lax.rem(h, 2) == 1))

    def relay(h, carry):
        for t in range(2):
            @pl.when(has_near)
            def _():
                near(h, t).wait_recv()

            @pl.when(sends_far(h))
            def _():
                far(h, t).start()

            @pl.when(has_near & (core == 0))
            def _():
                side_b(h, t).start()

            @pl.when(has_near & (core == 1))
            def _():
                side_a(h, t).start()

        @pl.when(detour_middle & (h >= kv_heads - kv_heads // 2))
        def _():
            for t in range(2):
                pass_in(h - (kv_heads - kv_heads // 2), t).wait_recv()
                pass_out(h - (kv_heads - kv_heads // 2), t).start()
        return carry

    lax.fori_loop(0, kv_heads, relay, 0)

    def attend(h, carry):
        for t in range(2):
            @pl.when(has_far)
            def _():
                far(h, t).wait_recv()

            @pl.when(has_far & (core == 1))
            def _():
                side_b(h, t).start()
        for t in range(2):
            @pl.when(has_near | (core == 1))
            def _():
                side_a(h, t).wait_recv()

            @pl.when(has_far | (has_near & (core == 1)))
            def _():
                side_b(h, t).wait_recv()
        key = k_ref[:, columns(h)]
        value = v_ref[:, columns(h)]
        for g in range(groups):
            head = pl.ds(pl.multiple_of((h * groups + g) * HD, HD), HD)
            scores = lax.dot_general(
                q_ref[:, head], key, (((1,), (1,)), ((), ())), preferred_element_type=jnp.float32)
            scores = scores * 0.0625 + bias_ref[...]
            top = jnp.max(scores, axis=1, keepdims=True)
            expo = jnp.exp(scores - top)
            total = jnp.sum(expo, axis=1, keepdims=True)
            mixed = jnp.dot(expo.astype(jnp.bfloat16), value, preferred_element_type=jnp.float32)
            out_ref[:, head] = (mixed / total).astype(out_ref.dtype)
        return carry

    lax.fori_loop(0, kv_heads, attend, 0)

    def drain(h, carry):
        for t in range(2):
            @pl.when(has_ahead)
            def _():
                near(h, t).wait_send()

            @pl.when(sends_far(h))
            def _():
                far(h, t).wait_send()

            @pl.when(has_near | (core == 0))
            def _():
                side_a(h, t).wait_send()

            @pl.when(has_far | (has_near & (core == 0)))
            def _():
                side_b(h, t).wait_send()

            @pl.when((detour_first | detour_middle) & (lax.rem(h, 2) == 1))
            def _():
                pass_in(lax.div(h, 2), t).wait_send()
        return carry

    lax.fori_loop(0, kv_heads, drain, 0)


def per_device(devices, queries, keys, values, doc_start):
    rows = queries.shape[0]
    kv_heads = keys.shape[1] // HD
    groups = queries.shape[1] // keys.shape[1]
    span = (HOPS + 1) * rows
    copies = pltpu.SemaphoreType.DMA((2 * kv_heads,))
    half = pltpu.SemaphoreType.DMA((kv_heads,))
    return pl.pallas_call(
        functools.partial(kernel, devices, rows, kv_heads, groups),
        out_shape=jax.ShapeDtypeStruct(queries.shape, jnp.bfloat16),
        in_specs=[pl.BlockSpec(memory_space=pltpu.HBM)] * 4,
        out_specs=pl.BlockSpec(memory_space=pltpu.VMEM),
        scratch_shapes=[
            pltpu.VMEM(queries.shape, jnp.bfloat16),
            pltpu.VMEM((span, keys.shape[1]), jnp.bfloat16),
            pltpu.VMEM((span, keys.shape[1]), jnp.bfloat16),
            pltpu.VMEM((rows, keys.shape[1] // 2), jnp.bfloat16),
            pltpu.VMEM((rows, keys.shape[1] // 2), jnp.bfloat16),
            pltpu.VMEM((1, rows), jnp.int32),
            pltpu.VMEM((rows, span), jnp.float32),
            copies, copies, copies, copies, copies, copies, copies, copies, copies, half, half,
            pltpu.SemaphoreType.DMA((2,)),
        ],
        compiler_params=pltpu.CompilerParams(
            collective_id=0, has_side_effects=True, vmem_limit_bytes=8 * 1024 * 1024),
    )(*(pltpu.with_memory_space_constraint(x, pltpu.HBM) for x in (queries, keys, values, doc_start.reshape(1, rows))))


def solution(mesh):
    return jax.shard_map(
        functools.partial(per_device, mesh.shape["blk"]),
        mesh=mesh,
        in_specs=(P("blk", None), P("blk", None), P("blk", None), P("blk")),
        out_specs=P("blk", None),
        check_vma=False,
    )
```

time: 44 us -> 40.9 us (0.930)
  the two profiles are of different devices: /device:TPU:1 before, /device:TPU:6 now
where the time goes in v2:
time: 40.9 us; the launch traced here: 40.8 us
  Pallas kernels  39.9 us (98%)
  local copies, waits for them, and re-layouts  0.8 us (2%)
    pallas_call x1, Pallas kernels, per_device(): pl.pallas_call(functools.partial(kernel, devices, rows, kv_heads, groups)...  39.9 us

profile of v2, /device:TPU:6, one launch (start us, length us, event | category | flops | bytes accessed | tf_op | source)
XLA Modules:
  0.0 40.8 jit_solution(14903985849285072709)
XLA Ops:
  0.0 39.9 %shard_map.46 = bf16[64,4096]{1,0:T(8,128)(2,1)S(1)} custom-call(bf16[64,4096]{1,0:T(8,128)(2,1)} %q_hbm.1, bf16[64,2048]{1,0:T(8,128)(2,1)} %k_hbm.1, bf16[64,2048]{1,0:T(8,128)(2,1)} %v_hbm.1, s32[1,64]{1,0:T(1,128)} %bitcast.1), custom_call_target="tpu_custom_call" | custom-call | tf_op jit(solution)/shard_map/pallas_call | solution.py:253
  40.0 0.8 %copy.6 = bf16[64,4096]{1,0:T(8,128)(2,1)} copy(bf16[64,4096]{1,0:T(8,128)(2,1)S(1)} %shard_map.46) | data formatting | bytes 1048576
